TPU v7x, 32 devices: a whole 2x2x4 slice. The times are simulated.
32 devices in a mesh: groups: 1, slab: 8 (over z, y), coil: 2 (over x), row: 2 (over core).
Axes of the slice: x: 2, y: 2, z: 4, core: 2. Of those that a mesh axis runs over, the one named last changes fastest.
Arguments:
- image: float32 [2, 128, 256, 128], P('groups', None, ('slab', 'row')), may hold values from -6 to 6
- sens: bfloat16 [2, 16, 128, 256, 128], P('groups', 'coil', None, ('slab', 'row')), may hold values from -1.5 to 1.5
- measured: bfloat16 [2, 16, 128, 256, 128], P('groups', 'coil', ('slab', 'row')), may hold values from -3 to 3
- mask: int32 [128, 256], P(('slab', 'row')), may hold values from 0 to 1, as said below
- thresholds: float32 [2, 7], replicated, may hold values from 0.1 to 1.5
Outputs:
- image_next: float32 [2, 128, 256, 128], P('groups', None, ('slab', 'row'))
Inputs may be any that keep to these rules, and one draw needn't show every extreme that they name: `mask`: A calibration block of the 8 central phase-encode lines (ky from 60 to 67) is sampled at every kz; outside it each (ky, kz) is sampled independently at random.
All inputs are finite; a program needn't handle non-finite values.
Results may differ from a plain program's by a relative error of at most 0.013.
Values may be sent and summed in bfloat16 or wider, within the bound.
A program may use at most 128 MiB of HBM per device.

v0:
```python
import functools
import math

import jax
import jax.numpy as jnp
import ml_dtypes
import numpy as np
from jax import lax
from jax.experimental import pallas as pl
from jax.experimental.pallas import tpu as pltpu
from jax.sharding import PartitionSpec as P

MESH = pl.DeviceIdType.MESH
half_root = 0.7071067811865476
quarter_root = 0.3535533905932738
step_size = 0.5
CALIBRATION = 8
LATE_COILS = 2


def fourier_table(length, sign):
    index = np.arange(length)
    theta = (index[:, None] * index[None, :] % length) * (2.0 * math.pi / length)
    real = np.cos(theta) / math.sqrt(length)
    imaginary = sign * np.sin(theta) / math.sqrt(length)
    return np.stack([np.stack([real, -imaginary]), np.stack([imaginary, real])])


def split_plane(plane, offset):
    cells_y, cells_x = plane.shape
    moved = pltpu.roll(plane, cells_x - offset, 1)
    bands = []
    for part in (plane + moved, plane - moved):
        bands.append((part, pltpu.roll(part, cells_y - offset, 0)))
    (low, low_moved), (high, high_moved) = bands
    return [low + low_moved, high + high_moved, low - low_moved, high - high_moved]


def merge_plane(bands, offset):
    across = []
    for lower, upper in ((bands[0], bands[2]), (bands[1], bands[3])):
        across.append(lower + upper + pltpu.roll(lower - upper, offset, 0))
    lower, upper = across
    return lower + upper + pltpu.roll(lower - upper, offset, 1)


def shrink_pair(real, imaginary, limit):
    factor = jnp.maximum(1.0 - limit * lax.rsqrt(real * real + imaginary * imaginary), 0.0)
    return real * factor, imaginary * factor


def wavelet_kernel(levels, planes, limits, source, result, *scratch):
    halo = 2**levels - 1
    stop = halo + planes
    coarse_refs = (source,) + scratch[: levels - 1]
    merged_refs = (None,) + scratch[levels - 1 : 2 * (levels - 1)]
    split_ref, carry_ref = scratch[2 * (levels - 1) :]
    extent = planes + 2 * halo
    for level in range(levels - 1):
        offset = 2**level
        extent -= offset
        finer, coarser = coarse_refs[level], coarse_refs[level + 1]

        def coarsen(n, _, offset=offset, finer=finer, coarser=coarser):
            for t in range(2):
                total = finer[t, n] + finer[t, n + offset]
                total = total + pltpu.roll(total, total.shape[1] - offset, 1)
                total = total + pltpu.roll(total, total.shape[0] - offset, 0)
                coarser[t, n] = total * half_root**3
            return 0

        lax.fori_loop(0, extent, coarsen, 0)
    for level in reversed(range(levels)):
        offset = 2**level
        slots = offset + 1
        first = halo - (offset - 1)
        start = first - offset
        coarse = coarse_refs[level]

        def enter(n, _, offset=offset, coarse=coarse, slots=slots):
            for t in range(2):
                for b, band in enumerate(split_plane(coarse[t, n] * half_root**3, offset)):
                    split_ref[lax.rem(n, slots), b, t] = band
            return 0

        lax.fori_loop(start, start + offset, enter, 0)

        def advance(n, _, level=level, offset=offset, slots=slots, first=first, enter=enter):
            enter(n + offset, 0)
            here, there, back = lax.rem(n, slots), lax.rem(n + offset, slots), lax.rem(n, offset)
            merged = [[], []]
            for b in range(4):
                near = [split_ref[here, b, t] for t in range(2)]
                far = [split_ref[there, b, t] for t in range(2)]
                high = shrink_pair(near[0] - far[0], near[1] - far[1], limits[level, b + 3])
                if b:
                    low = shrink_pair(near[0] + far[0], near[1] + far[1], limits[level, b - 1])
                elif level < levels - 1:
                    low = [merged_refs[level + 1][t, n] for t in range(2)]
                else:
                    low = (near[0] + far[0], near[1] + far[1])
                for t in range(2):
                    merged[t].append(low[t] + high[t] + carry_ref[back, b, t])
                    carry_ref[back, b, t] = low[t] - high[t]

            @pl.when(n >= first)
            def _():
                for t in range(2):
                    value = merge_plane(merged[t], offset) * quarter_root**3
                    if level:
                        merged_refs[level][t, n] = value
                    else:
                        result[t, n - halo] = value

            return 0

        lax.fori_loop(start, stop, advance, 0)


def wavelet_shrink(source, thresholds, planes):
    levels = thresholds.shape[0]
    halo = 2**levels - 1
    parts, _, cells_y, cells_x = source.shape
    plane = (cells_y, cells_x)
    store = [pltpu.VMEM((parts, planes + 2 * halo) + plane, jnp.float32)] * (2 * (levels - 1))
    whole = pl.BlockSpec(memory_space=pltpu.VMEM)
    return pl.pallas_call(
        functools.partial(wavelet_kernel, levels, planes),
        out_shape=jax.ShapeDtypeStruct((parts, planes) + plane, jnp.float32),
        in_specs=[pl.BlockSpec(memory_space=pltpu.SMEM), whole],
        out_specs=whole,
        scratch_shapes=store
        + [
            pltpu.VMEM((2 ** (levels - 1) + 1, 4, parts) + plane, jnp.float32),
            pltpu.VMEM((2 ** (levels - 1), 4, parts) + plane, jnp.float32),
        ],
        compiler_params=pltpu.CompilerParams(vmem_limit_bytes=32 * 2**20),
        name="wavelet",
    )(thresholds, source)


class Sizes:
    def __init__(self, image, sens, measured, thresholds, shards, coil_groups):
        self.shards, self.coil_groups = shards, coil_groups
        _, self.y, self.planes, self.x = image.shape
        self.z = measured.shape[3]
        self.coils = sens.shape[1]
        self.lines = self.y // shards
        self.part_lines = min(self.lines, 4)
        self.parts = self.lines // self.part_lines
        self.group = min(self.planes, 4)
        self.groups = self.planes // self.group
        self.halo = 2 ** thresholds.shape[0] - 1
        self.late = min(LATE_COILS, self.coils)
        self.early = self.coils - self.late
        first = self.y // 2 - CALIBRATION // 2
        self.calibration = (first, first + CALIBRATION)
        self.skipped = [
            [d for d in range(shards) if self.inside(d, h)] for h in range(self.parts)
        ]

    def inside(self, shard, part):
        start = shard * self.lines + part * self.part_lines
        return self.calibration[0] <= start and start + self.part_lines <= self.calibration[1]

    def is_skipped(self, shard, part):
        found = shard < 0
        for d in self.skipped[part]:
            found = found | (shard == d)
        return found


def tables(sizes):
    n, y, z, planes = sizes.shards, sizes.y, sizes.z, sizes.planes
    phase = fourier_table(y, -1.0)
    phase_rows = phase.reshape(2, 2, y, n, sizes.parts, sizes.part_lines)
    phase_rows = phase_rows.transpose(3, 4, 0, 5, 1, 2).reshape(2 * y, 2 * y)
    inverse = fourier_table(y, 1.0)
    inverse_rows = inverse.transpose(0, 3, 1, 2).reshape(2 * y, 2 * y)
    kept = np.zeros((y,))
    for h in range(sizes.parts):
        for d in sizes.skipped[h]:
            start = d * sizes.lines + h * sizes.part_lines
            kept[start : start + sizes.part_lines] = 1.0
    central = inverse * kept[None, None, :, None]
    central = central.reshape(2, 2, n, sizes.parts, sizes.part_lines, y)
    central = central.transpose(0, 5, 2, 3, 1, 4).reshape(2 * y, 2 * y)
    depth = fourier_table(z, -1.0).transpose(0, 3, 1, 2).reshape(2 * z, 2 * z)
    back = fourier_table(z, 1.0).reshape(2, 2, z, n, sizes.groups, sizes.group)
    back = back.transpose(3, 4, 0, 5, 1, 2).reshape(2 * z, 2 * z)
    readout = fourier_table(sizes.x, 1.0).transpose(1, 2, 0, 3).reshape(2 * sizes.x, 2 * sizes.x)
    found = (phase_rows, central, depth, back, inverse_rows, readout)
    return [jnp.asarray(t.astype(np.float32).astype(ml_dtypes.bfloat16)) for t in found]


def dot(left, right):
    return jnp.dot(left, right, preferred_element_type=jnp.float32)


def gradient_kernel(
    sizes, image, sens, measured, sampled, phase, central, depth, back, inverse, readout, source,
    out_f, in_f, out_b, in_b, sens_kept, wide, sens_slots, measured_slots, totals, edge_out, edge_in,
    sens_sem, measured_sem, out_f_sem, in_f_sem, out_b_sem, in_b_sem, out_q_sem, in_q_sem,
    total_out_sem, total_in_sem, edge_out_sem, edge_in_sem,
):
    n, x = sizes.shards, sizes.x
    coils, early, late = sizes.coils, sizes.early, sizes.late
    planes, halo, pair = sizes.planes, sizes.halo, 2
    rows_f = 2 * sizes.part_lines
    rows_b = 2 * sizes.group
    cells = sizes.y * planes
    rows_n = lax.axis_size("row")
    here = lax.axis_index("slab") * rows_n + lax.axis_index("row")
    scan, coil_here = lax.axis_index("groups"), lax.axis_index("coil")

    def device(shard, coil=None):
        return (scan, shard // rows_n, coil_here if coil is None else coil, lax.rem(shard, rows_n))

    def remote(src, dst, sent, got, target):
        return pltpu.make_async_remote_copy(
            src_ref=src, dst_ref=dst, send_sem=sent, recv_sem=got, device_id=target, device_id_type=MESH
        )

    def arrived(ref, sem):
        pltpu.make_async_copy(ref, ref, sem).wait()

    def sens_copy(c):
        slot = lax.rem(c, 2)
        return pltpu.make_async_copy(sens.at[:, c], sens_slots.at[slot], sens_sem.at[slot])

    def measured_copy(c):
        slot = lax.rem(c, 2)
        return pltpu.make_async_copy(measured.at[:, c], measured_slots.at[slot], measured_sem.at[slot])

    sens_copy(0).start()

    def forward(c, _):
        slot = lax.rem(c, 2)

        @pl.when(c + 1 < coils)
        def _():
            sens_copy(c + 1).start()

        sens_copy(c).wait()
        block = cells // 16

        def widen(i, _):
            at = pl.multiple_of(i * block, block)
            for t in range(2):
                wide[pl.ds(t * cells + at, block), :] = sens_slots[slot, t, pl.ds(at, block), :].astype(jnp.float32)
            return 0

        lax.fori_loop(0, 16, widen, 0)

        def plane(p, _):
            sr, si = (wide[pl.ds(t * cells + p, sizes.y, stride=planes), :] for t in range(2))
            ur, ui = (image[t, pl.ds(p, sizes.y, stride=planes), :] for t in range(2))
            sens_kept[c, 0, p] = sr.astype(jnp.bfloat16)
            sens_kept[c, 1, p] = si.astype(jnp.bfloat16)
            coil_image = jnp.concatenate([sr * ur - si * ui, sr * ui + si * ur], axis=0).astype(jnp.bfloat16)
            done = dot(phase[...], coil_image).reshape(n, sizes.parts, rows_f, x)
            out_f[c, :, :, p] = done.astype(jnp.bfloat16)
            return 0

        lax.fori_loop(0, planes, plane, 0)

        def send(d, _):
            to = lax.rem(here + d, n)
            for h in range(sizes.parts):

                @pl.when(jnp.logical_not(sizes.is_skipped(to, h)))
                def _():
                    remote(out_f.at[c, to, h], in_f.at[c, here, h], out_f_sem.at[c, h], in_f_sem.at[c, h], device(to)).start()

            return 0

        lax.fori_loop(1, n, send, 0)
        for h in range(sizes.parts):
            in_f[c, here, h] = out_f[c, here, h]

        def middle(p, _):
            lines = out_f[c, :, :, p].astype(jnp.float32).reshape(2 * sizes.y, x).astype(jnp.bfloat16)
            value = dot(central[...], lines)
            add_gradient(c, p, value[: sizes.y], value[sizes.y :], c == 0)
            return 0

        lax.fori_loop(0, planes, middle, 0)
        return 0

    def add_gradient(c, p, real, imaginary, fresh=None):
        sr = sens_kept[c, 0, p].astype(jnp.float32)
        si = sens_kept[c, 1, p].astype(jnp.float32)
        for t, term in ((0, sr * real + si * imaginary), (1, sr * imaginary - si * real)):
            held = source[t, halo + p]
            if fresh is not None:
                held = jnp.where(fresh, jnp.zeros_like(held), held)
            source[t, halo + p] = held + term

    lax.fori_loop(0, coils, forward, 0)

    measured_copy(0).start()

    def lines_of(c, _):
        slot = lax.rem(c, 2)

        @pl.when(c + 1 < coils)
        def _():
            measured_copy(c + 1).start()

        measured_copy(c).wait()
        for h in range(sizes.parts):
            skipped = sizes.is_skipped(here, h)

            @pl.when(jnp.logical_not(skipped))
            def _():
                arrived(in_f.at[c, pl.ds(0, n - 1), h], in_f_sem.at[c, h])

                def widen(i, _):
                    rows = planes * rows_f
                    at = pl.multiple_of(i * rows, rows)
                    wide[pl.ds(at, rows), :] = in_f[c, i, h].astype(jnp.float32).reshape(rows, x)
                    return 0

                lax.fori_loop(0, n, widen, 0)

            @pl.when(skipped)
            def _():
                def clear(i, _):
                    rows = planes * rows_f
                    wide[pl.ds(pl.multiple_of(i * rows, rows), rows), :] = jnp.zeros((rows, x), jnp.float32)
                    return 0

                lax.fori_loop(0, n, clear, 0)

            def two_lines(i, _):
                across = []
                for j in range(pair):
                    row = i * pair + j
                    parts = [wide[pl.ds(t * sizes.part_lines + row, sizes.z, stride=rows_f), :] for t in range(2)]
                    across.append(jnp.concatenate(parts, axis=0).astype(jnp.bfloat16))
                spectrum = dot(depth[...], jnp.concatenate(across, axis=1))
                residuals = []
                for j in range(pair):
                    line = h * sizes.part_lines + i * pair + j
                    both = jnp.concatenate([measured_slots[slot, t, line] for t in range(2)], axis=1)
                    data = dot(both, readout[...])
                    keep = sampled[line]
                    columns = slice(j * x, (j + 1) * x)
                    residuals.append(
                        jnp.concatenate(
                            [
                                keep * (spectrum[: sizes.z, columns] - data[:, :x]),
                                keep * (spectrum[sizes.z :, columns] - data[:, x:]),
                            ],
                            axis=0,
                        ).astype(jnp.bfloat16)
                    )
                returned = dot(back[...], jnp.concatenate(residuals, axis=1))
                for j in range(pair):
                    line = h * sizes.part_lines + i * pair + j
                    value = returned[:, j * x : (j + 1) * x].reshape(n, sizes.groups, rows_b, x)
                    out_b[c, :, :, line] = value.astype(jnp.bfloat16)
                return 0

            lax.fori_loop(0, sizes.part_lines // pair, two_lines, 0)

        in_b[c, here] = out_b[c, here]

        @pl.when(c < early)
        def _():
            def send(d, _):
                to = lax.rem(here + d, n)
                remote(out_b.at[c, to], in_b.at[c, here], out_b_sem.at[c], in_b_sem.at[c], device(to)).start()
                return 0

            lax.fori_loop(1, n, send, 0)

        return 0

    lax.fori_loop(0, coils, lines_of, 0)
    order = [0] + ([sizes.groups - 1] if sizes.groups > 1 else []) + list(range(1, sizes.groups - 1))
    last = pl.ds(early, late)
    for q in order:

        def send(d, _, q=q):
            to = lax.rem(here + d, n)
            remote(out_b.at[last, to, q], in_b.at[last, here, q], out_q_sem.at[q], in_q_sem.at[q], device(to)).start()
            return 0

        lax.fori_loop(1, n, send, 0)

    def combine(c, q):
        rows = sizes.lines * rows_b

        def widen(i, _):
            at = pl.multiple_of(i * rows, rows)
            wide[pl.ds(at, rows), :] = in_b[c, i, q].astype(jnp.float32).reshape(rows, x)
            return 0

        lax.fori_loop(0, n, widen, 0)

        def two_planes(i, _):
            across = []
            for j in range(pair):
                row = i * pair + j
                parts = [wide[pl.ds(t * sizes.group + row, sizes.y, stride=rows_b), :] for t in range(2)]
                across.append(jnp.concatenate(parts, axis=0).astype(jnp.bfloat16))
            value = dot(inverse[...], jnp.concatenate(across, axis=1))
            for j in range(pair):
                columns = slice(j * x, (j + 1) * x)
                add_gradient(c, q * sizes.group + i * pair + j, value[: sizes.y, columns], value[sizes.y :, columns])
            return 0

        lax.fori_loop(0, sizes.group // pair, two_planes, 0)

    def early_coil(c, _):
        arrived(in_b.at[c, pl.ds(0, n - 1)], in_b_sem.at[c])

        def each(q, _):
            combine(c, q)
            return 0

        lax.fori_loop(0, sizes.groups, each, 0)
        return 0

    lax.fori_loop(0, early, early_coil, 0)

    def total_copy(q, distance):
        to = lax.rem(coil_here + distance, sizes.coil_groups)
        return remote(
            totals.at[coil_here, q], totals.at[coil_here, q], total_out_sem.at[q, distance - 1],
            total_in_sem.at[q, distance - 1], device(here, to),
        )

    def finish(q):
        for distance in range(1, sizes.coil_groups):
            total_copy(q, distance).wait_recv()

        def plane(i, _):
            p = q * sizes.group + i
            for t in range(2):
                total = totals[0, q, t, i].astype(jnp.float32)
                for k in range(1, sizes.coil_groups):
                    total = total + totals[k, q, t, i].astype(jnp.float32)
                source[t, halo + p] = image[t, pl.ds(p, sizes.y, stride=planes), :] - step_size * total
            return 0

        lax.fori_loop(0, sizes.group, plane, 0)

    def edge_copy(side):
        to = lax.rem(here + (1, n - 1)[side], n)
        return remote(edge_out.at[side], edge_in.at[side], edge_out_sem.at[side], edge_in_sem.at[side], device(to))

    ends = set(order[:2])
    for step, q in enumerate(order):
        arrived(in_b.at[last, pl.ds(0, n - 1), q], in_q_sem.at[q])

        def each(c, _, q=q):
            combine(early + c, q)
            return 0

        lax.fori_loop(0, late, each, 0)
        for t in range(2):
            for i in range(sizes.group):
                totals[coil_here, q, t, i] = source[t, halo + q * sizes.group + i].astype(jnp.bfloat16)
        for distance in range(1, sizes.coil_groups):
            total_copy(q, distance).start()
        done = order[:step] if step else []
        if done:
            finish(done[-1])
        if ends.issubset(done) and not ends.issubset(done[:-1]):
            exchange_edges = True
        else:
            exchange_edges = False
        if exchange_edges:
            for t in range(2):
                edge_out[0, t] = source[t, planes : planes + halo].astype(jnp.bfloat16)
                edge_out[1, t] = source[t, halo : 2 * halo].astype(jnp.bfloat16)
            for side in range(2):
                edge_copy(side).start()
    finish(order[-1])
    if not ends.issubset(order[:-1]):
        for t in range(2):
            edge_out[0, t] = source[t, planes : planes + halo].astype(jnp.bfloat16)
            edge_out[1, t] = source[t, halo : 2 * halo].astype(jnp.bfloat16)
        for side in range(2):
            edge_copy(side).start()
    for side in range(2):
        edge_copy(side).wait_recv()
    for t in range(2):
        source[t, :halo] = edge_in[0, t].astype(jnp.float32)
        source[t, halo + planes :] = edge_in[1, t].astype(jnp.float32)

    for side in range(2):
        edge_copy(side).wait_send()
    for q in order:
        arrived(out_b.at[last, pl.ds(0, n - 1), q], out_q_sem.at[q])
        for distance in range(1, sizes.coil_groups):
            total_copy(q, distance).wait_send()

    def left(c, _):
        for h in range(sizes.parts):
            skipped = sizes.is_skipped(here, h)
            others = n - len(sizes.skipped[h])

            @pl.when(skipped)
            def _():
                arrived(out_f.at[c, pl.ds(0, others), h], out_f_sem.at[c, h])

            @pl.when(jnp.logical_not(skipped))
            def _():
                arrived(out_f.at[c, pl.ds(0, others - 1), h], out_f_sem.at[c, h])

        @pl.when(c < early)
        def _():
            arrived(out_b.at[c, pl.ds(0, n - 1)], out_b_sem.at[c])

        return 0

    lax.fori_loop(0, coils, left, 0)


def descent_planes(image, sens, measured, mask, thresholds):
    sizes = Sizes(image, sens, measured, thresholds, lax.axis_size(("slab", "row")), lax.axis_size("coil"))
    n, x, y, planes, coils = sizes.shards, sizes.x, sizes.y, sizes.planes, sizes.coils
    cells = y * planes
    sampled = jnp.broadcast_to(mask.astype(jnp.float32)[:, :, None], mask.shape + (x,))
    forward = (coils, n, sizes.parts, planes, 2 * sizes.part_lines, x)
    backward = (coils, n, sizes.groups, sizes.lines, 2 * sizes.group, x)
    bf, dma = jnp.bfloat16, pltpu.SemaphoreType.DMA
    rows = max(2 * cells, n * planes * 2 * sizes.part_lines, y * 2 * sizes.group)
    whole, anywhere = pl.BlockSpec(memory_space=pltpu.VMEM), pl.BlockSpec(memory_space=pl.ANY)
    others = max(sizes.coil_groups - 1, 1)
    return pl.pallas_call(
        functools.partial(gradient_kernel, sizes),
        out_shape=jax.ShapeDtypeStruct((2, planes + 2 * sizes.halo, y, x), jnp.float32),
        in_specs=[whole, anywhere, anywhere] + [whole] * 7,
        out_specs=whole,
        scratch_shapes=[
            pltpu.VMEM(forward, bf),
            pltpu.VMEM(forward, bf),
            pltpu.VMEM(backward, bf),
            pltpu.VMEM(backward, bf),
            pltpu.VMEM((coils, 2, planes, y, x), bf),
            pltpu.VMEM((rows, x), jnp.float32),
            pltpu.VMEM((2, 2, cells, x), bf),
            pltpu.VMEM((2, 2, sizes.lines, sizes.z, x), bf),
            pltpu.VMEM((sizes.coil_groups, sizes.groups, 2, sizes.group, y, x), bf),
            pltpu.VMEM((2, 2, sizes.halo, y, x), bf),
            pltpu.VMEM((2, 2, sizes.halo, y, x), bf),
            dma((2,)),
            dma((2,)),
            dma((coils, sizes.parts)),
            dma((coils, sizes.parts)),
            dma((coils,)),
            dma((coils,)),
            dma((sizes.groups,)),
            dma((sizes.groups,)),
            dma((sizes.groups, others)),
            dma((sizes.groups, others)),
            dma((2,)),
            dma((2,)),
        ],
        compiler_params=pltpu.CompilerParams(has_side_effects=True, vmem_limit_bytes=67043328),
        name="gradient",
    )(image.reshape(2, cells, x), sens.reshape(2, coils, cells, x), measured, sampled, *tables(sizes))


def shrinkage_step(image, sens, measured, mask, thresholds):
    source = descent_planes(image, sens, measured, mask, thresholds)
    return jnp.swapaxes(wavelet_shrink(source, thresholds, image.shape[2]), 1, 2)


def solution(mesh):
    return jax.shard_map(
        shrinkage_step,
        mesh=mesh,
        in_specs=(
            P("groups", None, ("slab", "row"), None),
            P("groups", "coil", None, ("slab", "row"), None),
            P("groups", "coil", ("slab", "row"), None, None),
            P(("slab", "row"), None),
            P(),
        ),
        out_specs=P("groups", None, ("slab", "row"), None),
        check_vma=False,
    )
```

profile of v0, /device:TPU:28, one launch (start us, length us, event | category | flops | bytes accessed | tf_op | source)
XLA Modules:
  0.0 407.4 jit_solution(16770060015354363271)
XLA Ops:
  0.0 0.7 convert_element_type.3
  0.7 1.3 broadcast_in_dim.2.sampled
  2.0 378.7 %gradient.1.source = f32[2,22,128,128]{3,2,1,0:T(8,128)} custom-call(f32[2,2048,128]{2,1,0:T(8,128)} %bitcast.5, bf16[2,8,2048,128]{3,2,1,0:T(8,128)(2,1)} %bitcast.4, bf16[2,8,8,256,128]{4,3,2,1,0:T(8,128)(2,1)} %measured.1, f32[8,256,128]{2,1,0:T(8,128)} %broadcast_in_dim.2.sampled, bf16[256,256]{1,0:T(8,128)(2,1)} %constant.12.clone.phase, ...), custom_call_target="tpu_custom_call" | custom-call | tf_op jit(solution)/shard_map/gradient/pallas_call | solution.py:534
  380.7 0.0 copy-start
  380.7 1.8 copy-done
  382.5 0.0 copy-start.1
  382.5 0.7 copy-done.1
  383.2 21.7 %wavelet.1 = f32[2,16,128,128]{3,2,1,0:T(8,128)S(1)} custom-call(f32[2,7]{1,0:T(2,128)S(1)} %copy-done.1, f32[2,22,128,128]{3,2,1,0:T(8,128)S(1)} %copy-done), custom_call_target="tpu_custom_call" | custom-call | tf_op jit(solution)/shard_map/wavelet/pallas_call | solution.py:127
  404.9 2.5 copy.12
Async XLA Ops:
  380.7 1.8 copy-start
  382.5 0.7 copy-start.1
where the time goes:
time: 408 us; the launch traced here: 407 us
  Pallas kernels  400 us (98%)
  local copies, waits for them, and re-layouts  6.33 us (2%)
    pallas_call x1, Pallas kernels, descent_planes(): pl.pallas_call(functools.partial(gradient_kernel, sizes), out_shape=jax.S...  379 us
    pallas_call x1, Pallas kernels, wavelet_shrink(): pl.pallas_call(functools.partial(wavelet_kernel, levels, planes), out_sha...  21.7 us

commit v1 on v0

--- a/solution.py
+++ b/solution.py
@@ -11,8 +11,6 @@
 from jax.sharding import PartitionSpec as P
 
 MESH = pl.DeviceIdType.MESH
-half_root = 0.7071067811865476
-quarter_root = 0.3535533905932738
 step_size = 0.5
 CALIBRATION = 8
 LATE_COILS = 2
@@ -26,22 +24,23 @@
     return np.stack([np.stack([real, -imaginary]), np.stack([imaginary, real])])
 
 
-def split_plane(plane, offset):
-    cells_y, cells_x = plane.shape
-    moved = pltpu.roll(plane, cells_x - offset, 1)
-    bands = []
-    for part in (plane + moved, plane - moved):
-        bands.append((part, pltpu.roll(part, cells_y - offset, 0)))
-    (low, low_moved), (high, high_moved) = bands
-    return [low + low_moved, high + high_moved, low - low_moved, high - high_moved]
-
-
-def merge_plane(bands, offset):
-    across = []
-    for lower, upper in ((bands[0], bands[2]), (bands[1], bands[3])):
-        across.append(lower + upper + pltpu.roll(lower - upper, offset, 0))
-    lower, upper = across
-    return lower + upper + pltpu.roll(lower - upper, offset, 1)
+GUARD = 8
+
+
+def split_plane(read, write, across, offset):
+    cells_y, cells_x = across.shape[2] - GUARD, across.shape[3]
+    for t in range(2):
+        value = read(t)
+        moved = pltpu.roll(value, cells_x - offset, 1)
+        for b, part in ((0, value + moved), (1, value - moved)):
+            across[b, t, :cells_y, :] = part
+            across[b, t, cells_y:, :] = part[:GUARD]
+    for b in range(2):
+        for t in range(2):
+            value = across[b, t, :cells_y, :]
+            moved = across[b, t, offset : offset + cells_y, :]
+            write(b, t, value + moved)
+            write(b + 2, t, value - moved)
 
 
 def shrink_pair(real, imaginary, limit):
@@ -49,69 +48,78 @@
     return real * factor, imaginary * factor
 
 
-def wavelet_kernel(levels, planes, limits, source, result, *scratch):
+def wavelet_kernel(levels, planes, limits, descent, result, source, across, kept, moved, carry, source_sem, *bands_of):
     halo = 2**levels - 1
     stop = halo + planes
-    coarse_refs = (source,) + scratch[: levels - 1]
-    merged_refs = (None,) + scratch[levels - 1 : 2 * (levels - 1)]
-    split_ref, carry_ref = scratch[2 * (levels - 1) :]
+    cells_y, cells_x = source.shape[2:]
     extent = planes + 2 * halo
-    for level in range(levels - 1):
+
+    def plane_copy(n):
+        return pltpu.make_async_copy(descent.at[:, n], source.at[:, n], source_sem.at[n])
+
+    def fetch(n, _):
+        plane_copy(n).start()
+        return 0
+
+    lax.fori_loop(0, extent, fetch, 0)
+    for level in range(levels):
         offset = 2**level
-        extent -= offset
-        finer, coarser = coarse_refs[level], coarse_refs[level + 1]
-
-        def coarsen(n, _, offset=offset, finer=finer, coarser=coarser):
-            for t in range(2):
-                total = finer[t, n] + finer[t, n + offset]
-                total = total + pltpu.roll(total, total.shape[1] - offset, 1)
-                total = total + pltpu.roll(total, total.shape[0] - offset, 0)
-                coarser[t, n] = total * half_root**3
-            return 0
-
-        lax.fori_loop(0, extent, coarsen, 0)
+        bands, finer = bands_of[level], bands_of[level - 1] if level else None
+
+        def split(n, _, offset=offset, bands=bands, finer=finer, reach=2 ** (level - 1) if level else 0):
+            if finer is None:
+                plane_copy(n).wait()
+
+            def read(t):
+                if finer is None:
+                    return source[t, n]
+                return finer[n, 0, t, :cells_y, :] + finer[n + reach, 0, t, :cells_y, :]
+
+            def write(b, t, value):
+                bands[n, b, t, :cells_y, :] = value
+
+            split_plane(read, write, across, offset)
+            return 0
+
+        if level:
+            extent -= 2 ** (level - 1)
+        lax.fori_loop(0, extent, split, 0)
     for level in reversed(range(levels)):
         offset = 2**level
-        slots = offset + 1
         first = halo - (offset - 1)
         start = first - offset
-        coarse = coarse_refs[level]
-
-        def enter(n, _, offset=offset, coarse=coarse, slots=slots):
-            for t in range(2):
-                for b, band in enumerate(split_plane(coarse[t, n] * half_root**3, offset)):
-                    split_ref[lax.rem(n, slots), b, t] = band
-            return 0
-
-        lax.fori_loop(start, start + offset, enter, 0)
-
-        def advance(n, _, level=level, offset=offset, slots=slots, first=first, enter=enter):
-            enter(n + offset, 0)
-            here, there, back = lax.rem(n, slots), lax.rem(n + offset, slots), lax.rem(n, offset)
+        bands, last = bands_of[level], level == levels - 1
+        scale = (2.0 * 2.0**0.5) ** (level + 1)
+
+        def advance(n, _, level=level, offset=offset, first=first, bands=bands, last=last, scale=scale):
+            back = lax.rem(n, offset)
             merged = [[], []]
             for b in range(4):
-                near = [split_ref[here, b, t] for t in range(2)]
-                far = [split_ref[there, b, t] for t in range(2)]
-                high = shrink_pair(near[0] - far[0], near[1] - far[1], limits[level, b + 3])
+                near = [bands[n, b, t, :cells_y, :] for t in range(2)]
+                far = [bands[n + offset, b, t, :cells_y, :] for t in range(2)]
+                high = shrink_pair(near[0] - far[0], near[1] - far[1], limits[level, b + 3] * scale)
                 if b:
-                    low = shrink_pair(near[0] + far[0], near[1] + far[1], limits[level, b - 1])
-                elif level < levels - 1:
-                    low = [merged_refs[level + 1][t, n] for t in range(2)]
+                    low = shrink_pair(near[0] + far[0], near[1] + far[1], limits[level, b - 1] * scale)
+                elif last:
+                    low = [near[t] + far[t] for t in range(2)]
                 else:
-                    low = (near[0] + far[0], near[1] + far[1])
+                    low = [bands_of[level + 1][n, 0, t, :cells_y, :] for t in range(2)]
                 for t in range(2):
-                    merged[t].append(low[t] + high[t] + carry_ref[back, b, t])
-                    carry_ref[back, b, t] = low[t] - high[t]
-
-            @pl.when(n >= first)
-            def _():
-                for t in range(2):
-                    value = merge_plane(merged[t], offset) * quarter_root**3
-                    if level:
-                        merged_refs[level][t, n] = value
-                    else:
-                        result[t, n - halo] = value
-
+                    merged[t].append(low[t] + high[t] + carry[back, b, t, :cells_y, :])
+                    carry[back, b, t, :cells_y, :] = low[t] - high[t]
+            for t in range(2):
+                for b in range(2):
+                    kept[b, t, :cells_y, :] = merged[t][b] + merged[t][b + 2]
+                    turned = merged[t][b] - merged[t][b + 2]
+                    moved[b, t, GUARD:, :] = turned
+                    moved[b, t, :GUARD, :] = turned[cells_y - GUARD :]
+            for t in range(2):
+                low, high = (kept[b, t, :cells_y, :] + moved[b, t, GUARD - offset : GUARD - offset + cells_y, :] for b in range(2))
+                value = (low + high + pltpu.roll(low - high, offset, 1)) * 0.015625
+                if level:
+                    bands[n, 0, t, :cells_y, :] = value
+                else:
+                    result[t, pl.ds(jnp.maximum(n - halo, 0), cells_y, stride=planes), :] = value
             return 0
 
         lax.fori_loop(start, stop, advance, 0)
@@ -121,20 +129,24 @@
     levels = thresholds.shape[0]
     halo = 2**levels - 1
     parts, _, cells_y, cells_x = source.shape
-    plane = (cells_y, cells_x)
-    store = [pltpu.VMEM((parts, planes + 2 * halo) + plane, jnp.float32)] * (2 * (levels - 1))
+    plane = (cells_y + GUARD, cells_x)
+    guarded = pltpu.VMEM((2, parts) + plane, jnp.float32)
     whole = pl.BlockSpec(memory_space=pltpu.VMEM)
     return pl.pallas_call(
         functools.partial(wavelet_kernel, levels, planes),
-        out_shape=jax.ShapeDtypeStruct((parts, planes) + plane, jnp.float32),
-        in_specs=[pl.BlockSpec(memory_space=pltpu.SMEM), whole],
+        out_shape=jax.ShapeDtypeStruct((parts, cells_y * planes, cells_x), jnp.float32),
+        in_specs=[pl.BlockSpec(memory_space=pltpu.SMEM), pl.BlockSpec(memory_space=pltpu.HBM)],
         out_specs=whole,
-        scratch_shapes=store
-        + [
-            pltpu.VMEM((2 ** (levels - 1) + 1, 4, parts) + plane, jnp.float32),
+        scratch_shapes=[
+            pltpu.VMEM(source.shape, jnp.float32),
+            guarded,
+            guarded,
+            guarded,
             pltpu.VMEM((2 ** (levels - 1), 4, parts) + plane, jnp.float32),
-        ],
-        compiler_params=pltpu.CompilerParams(vmem_limit_bytes=32 * 2**20),
+            pltpu.SemaphoreType.DMA((planes + 2 * halo,)),
+        ]
+        + [pltpu.VMEM((planes + 2 * halo, 4, parts) + plane, jnp.float32)] * levels,
+        compiler_params=pltpu.CompilerParams(vmem_limit_bytes=60 * 2**20),
         name="wavelet",
     )(thresholds, source)
 
@@ -198,8 +210,8 @@
 
 
 def gradient_kernel(
-    sizes, image, sens, measured, sampled, phase, central, depth, back, inverse, readout, source,
-    out_f, in_f, out_b, in_b, sens_kept, wide, sens_slots, measured_slots, totals, edge_out, edge_in,
+    sizes, image, sens, measured, mask, phase, central, depth, back, inverse, readout, source,
+    out_f, in_f, out_b, in_b, sens_kept, wide, sampled, sens_slots, measured_slots, totals, edge_out, edge_in,
     sens_sem, measured_sem, out_f_sem, in_f_sem, out_b_sem, in_b_sem, out_q_sem, in_q_sem,
     total_out_sem, total_in_sem, edge_out_sem, edge_in_sem,
 ):
@@ -234,7 +246,7 @@
 
     sens_copy(0).start()
 
-    def forward(c, _):
+    def forward(c, pieces):
         slot = lax.rem(c, 2)
 
         @pl.when(c + 1 < coils)
@@ -262,19 +274,29 @@
             out_f[c, :, :, p] = done.astype(jnp.bfloat16)
             return 0
 
-        lax.fori_loop(0, planes, plane, 0)
-
-        def send(d, _):
-            to = lax.rem(here + d, n)
-            for h in range(sizes.parts):
-
-                @pl.when(jnp.logical_not(sizes.is_skipped(to, h)))
-                def _():
-                    remote(out_f.at[c, to, h], in_f.at[c, here, h], out_f_sem.at[c, h], in_f_sem.at[c, h], device(to)).start()
-
-            return 0
-
-        lax.fori_loop(1, n, send, 0)
+        share = planes // pieces
+
+        def piece(k, _):
+            lax.fori_loop(k * share, (k + 1) * share, plane, 0)
+            taken = pl.ds(k * share, share)
+
+            def send(d, _):
+                to = lax.rem(here + d, n)
+                for h in range(sizes.parts):
+
+                    @pl.when(jnp.logical_not(sizes.is_skipped(to, h)))
+                    def _():
+                        remote(
+                            out_f.at[c, to, h, taken], in_f.at[c, here, h, taken],
+                            out_f_sem.at[c, h], in_f_sem.at[c, h], device(to),
+                        ).start()
+
+                return 0
+
+            lax.fori_loop(1, n, send, 0)
+            return 0
+
+        lax.fori_loop(0, pieces, piece, 0)
         for h in range(sizes.parts):
             in_f[c, here, h] = out_f[c, here, h]
 
@@ -296,9 +318,16 @@
                 held = jnp.where(fresh, jnp.zeros_like(held), held)
             source[t, halo + p] = held + term
 
-    lax.fori_loop(0, coils, forward, 0)
+    forward(jnp.int32(0), math.gcd(planes, 4))
+    lax.fori_loop(1, coils, lambda c, _: forward(c, 1), 0)
 
     measured_copy(0).start()
+    kept = mask[...].astype(jnp.float32)
+    if sizes.lines % 8:
+        kept = jnp.concatenate([kept, jnp.zeros((8 - sizes.lines % 8, sizes.z), jnp.float32)], axis=0)
+    kept = kept.T
+    for line in range(sizes.lines):
+        sampled[line] = jnp.broadcast_to(kept[:, line : line + 1], (sizes.z, x))
 
     def lines_of(c, _):
         slot = lax.rem(c, 2)
@@ -389,35 +418,36 @@
 
         lax.fori_loop(1, n, send, 0)
 
-    def combine(c, q):
+    area = sizes.y * rows_b
+
+    def widen_back(c, q, base):
         rows = sizes.lines * rows_b
 
         def widen(i, _):
-            at = pl.multiple_of(i * rows, rows)
+            at = pl.multiple_of(base + i * rows, rows)
             wide[pl.ds(at, rows), :] = in_b[c, i, q].astype(jnp.float32).reshape(rows, x)
             return 0
 
         lax.fori_loop(0, n, widen, 0)
 
-        def two_planes(i, _):
-            across = []
-            for j in range(pair):
-                row = i * pair + j
-                parts = [wide[pl.ds(t * sizes.group + row, sizes.y, stride=rows_b), :] for t in range(2)]
-                across.append(jnp.concatenate(parts, axis=0).astype(jnp.bfloat16))
-            value = dot(inverse[...], jnp.concatenate(across, axis=1))
-            for j in range(pair):
-                columns = slice(j * x, (j + 1) * x)
-                add_gradient(c, q * sizes.group + i * pair + j, value[: sizes.y, columns], value[sizes.y :, columns])
-            return 0
-
-        lax.fori_loop(0, sizes.group // pair, two_planes, 0)
+    def two_planes(c, q, i, base):
+        across = []
+        for j in range(pair):
+            row = base + i * pair + j
+            parts = [wide[pl.ds(t * sizes.group + row, sizes.y, stride=rows_b), :] for t in range(2)]
+            across.append(jnp.concatenate(parts, axis=0).astype(jnp.bfloat16))
+        value = dot(inverse[...], jnp.concatenate(across, axis=1))
+        for j in range(pair):
+            columns = slice(j * x, (j + 1) * x)
+            add_gradient(c, q * sizes.group + i * pair + j, value[: sizes.y, columns], value[sizes.y :, columns])
 
     def early_coil(c, _):
         arrived(in_b.at[c, pl.ds(0, n - 1)], in_b_sem.at[c])
 
         def each(q, _):
-            combine(c, q)
+            widen_back(c, q, 0)
+            for i in range(sizes.group // pair):
+                two_planes(c, q, i, 0)
             return 0
 
         lax.fori_loop(0, sizes.groups, each, 0)
@@ -425,27 +455,35 @@
 
     lax.fori_loop(0, early, early_coil, 0)
 
-    def total_copy(q, distance):
+    def total_copy(q, i, distance):
         to = lax.rem(coil_here + distance, sizes.coil_groups)
-        return remote(
-            totals.at[coil_here, q], totals.at[coil_here, q], total_out_sem.at[q, distance - 1],
-            total_in_sem.at[q, distance - 1], device(here, to),
-        )
+        ref = totals.at[coil_here, q, i]
+        return remote(ref, ref, total_out_sem.at[q, i, distance - 1], total_in_sem.at[q, i, distance - 1], device(here, to))
+
+    def late_group(q):
+        for c in range(late):
+            widen_back(early + c, q, c * area)
+        for i in range(sizes.group // pair):
+            for c in range(late):
+                two_planes(early + c, q, i, c * area)
+            for t in range(2):
+                for j in range(pair):
+                    value = source[t, halo + q * sizes.group + i * pair + j]
+                    totals[coil_here, q, i, t, j] = value.astype(jnp.bfloat16)
+            for distance in range(1, sizes.coil_groups):
+                total_copy(q, i, distance).start()
 
     def finish(q):
-        for distance in range(1, sizes.coil_groups):
-            total_copy(q, distance).wait_recv()
-
-        def plane(i, _):
-            p = q * sizes.group + i
-            for t in range(2):
-                total = totals[0, q, t, i].astype(jnp.float32)
-                for k in range(1, sizes.coil_groups):
-                    total = total + totals[k, q, t, i].astype(jnp.float32)
-                source[t, halo + p] = image[t, pl.ds(p, sizes.y, stride=planes), :] - step_size * total
-            return 0
-
-        lax.fori_loop(0, sizes.group, plane, 0)
+        for i in range(sizes.group // pair):
+            for distance in range(1, sizes.coil_groups):
+                total_copy(q, i, distance).wait_recv()
+            for j in range(pair):
+                p = q * sizes.group + i * pair + j
+                for t in range(2):
+                    total = totals[0, q, i, t, j].astype(jnp.float32)
+                    for k in range(1, sizes.coil_groups):
+                        total = total + totals[k, q, i, t, j].astype(jnp.float32)
+                    source[t, halo + p] = image[t, pl.ds(p, sizes.y, stride=planes), :] - step_size * total
 
     def edge_copy(side):
         to = lax.rem(here + (1, n - 1)[side], n)
@@ -455,16 +493,7 @@
     for step, q in enumerate(order):
         arrived(in_b.at[last, pl.ds(0, n - 1), q], in_q_sem.at[q])
 
-        def each(c, _, q=q):
-            combine(early + c, q)
-            return 0
-
-        lax.fori_loop(0, late, each, 0)
-        for t in range(2):
-            for i in range(sizes.group):
-                totals[coil_here, q, t, i] = source[t, halo + q * sizes.group + i].astype(jnp.bfloat16)
-        for distance in range(1, sizes.coil_groups):
-            total_copy(q, distance).start()
+        late_group(q)
         done = order[:step] if step else []
         if done:
             finish(done[-1])
@@ -496,7 +525,8 @@
     for q in order:
         arrived(out_b.at[last, pl.ds(0, n - 1), q], out_q_sem.at[q])
         for distance in range(1, sizes.coil_groups):
-            total_copy(q, distance).wait_send()
+            for i in range(sizes.group // pair):
+                total_copy(q, i, distance).wait_send()
 
     def left(c, _):
         for h in range(sizes.parts):
@@ -524,11 +554,10 @@
     sizes = Sizes(image, sens, measured, thresholds, lax.axis_size(("slab", "row")), lax.axis_size("coil"))
     n, x, y, planes, coils = sizes.shards, sizes.x, sizes.y, sizes.planes, sizes.coils
     cells = y * planes
-    sampled = jnp.broadcast_to(mask.astype(jnp.float32)[:, :, None], mask.shape + (x,))
     forward = (coils, n, sizes.parts, planes, 2 * sizes.part_lines, x)
     backward = (coils, n, sizes.groups, sizes.lines, 2 * sizes.group, x)
     bf, dma = jnp.bfloat16, pltpu.SemaphoreType.DMA
-    rows = max(2 * cells, n * planes * 2 * sizes.part_lines, y * 2 * sizes.group)
+    rows = max(2 * cells, n * planes * 2 * sizes.part_lines, sizes.late * y * 2 * sizes.group)
     whole, anywhere = pl.BlockSpec(memory_space=pltpu.VMEM), pl.BlockSpec(memory_space=pl.ANY)
     others = max(sizes.coil_groups - 1, 1)
     return pl.pallas_call(
@@ -543,9 +572,10 @@
             pltpu.VMEM(backward, bf),
             pltpu.VMEM((coils, 2, planes, y, x), bf),
             pltpu.VMEM((rows, x), jnp.float32),
+            pltpu.VMEM((sizes.lines, sizes.z, x), jnp.float32),
             pltpu.VMEM((2, 2, cells, x), bf),
             pltpu.VMEM((2, 2, sizes.lines, sizes.z, x), bf),
-            pltpu.VMEM((sizes.coil_groups, sizes.groups, 2, sizes.group, y, x), bf),
+            pltpu.VMEM((sizes.coil_groups, sizes.groups, sizes.group // 2, 2, 2, y, x), bf),
             pltpu.VMEM((2, 2, sizes.halo, y, x), bf),
             pltpu.VMEM((2, 2, sizes.halo, y, x), bf),
             dma((2,)),
@@ -556,19 +586,19 @@
             dma((coils,)),
             dma((sizes.groups,)),
             dma((sizes.groups,)),
-            dma((sizes.groups, others)),
-            dma((sizes.groups, others)),
+            dma((sizes.groups, sizes.group // 2, others)),
+            dma((sizes.groups, sizes.group // 2, others)),
             dma((2,)),
             dma((2,)),
         ],
         compiler_params=pltpu.CompilerParams(has_side_effects=True, vmem_limit_bytes=67043328),
         name="gradient",
-    )(image.reshape(2, cells, x), sens.reshape(2, coils, cells, x), measured, sampled, *tables(sizes))
+    )(image.reshape(2, cells, x), sens.reshape(2, coils, cells, x), measured, mask, *tables(sizes))
 
 
 def shrinkage_step(image, sens, measured, mask, thresholds):
     source = descent_planes(image, sens, measured, mask, thresholds)
-    return jnp.swapaxes(wavelet_shrink(source, thresholds, image.shape[2]), 1, 2)
+    return wavelet_shrink(source, thresholds, image.shape[2]).reshape(image.shape)
 
 
 def solution(mesh):

time: 408 us -> 397 us (0.973)
  local copies, waits for them, and re-layouts: 6.33 us -> 0 us
    pallas_call x1, Pallas kernels: 379 us -> 374 us  [descent_planes(): pl.pallas_call(functools.partial(gradient_kernel, sizes), out_shape=jax.S...]
where the time goes in v1:
time: 397 us
  Pallas kernels  397 us (100%)
    pallas_call x1, Pallas kernels, descent_planes(): pl.pallas_call(functools.partial(gradient_kernel, sizes), out_shape=jax.S...  374 us
    pallas_call x1, Pallas kernels, wavelet_shrink(): pl.pallas_call(functools.partial(wavelet_kernel, levels, planes), out_sha...  23 us

profile of v1, /device:TPU:28, one launch (start us, length us, event | category | flops | bytes accessed | tf_op | source)
XLA Modules:
  0.0 397.2 jit_solution(10301500202795107081)
XLA Ops:
  0.0 374.1 %gradient.1.descent = f32[2,22,128,128]{3,2,1,0:T(8,128)} custom-call(f32[2,2048,128]{2,1,0:T(8,128)} %bitcast.4, bf16[2,8,2048,128]{3,2,1,0:T(8,128)(2,1)} %bitcast.3, bf16[2,8,8,256,128]{4,3,2,1,0:T(8,128)(2,1)} %measured.1, s32[8,256]{1,0:T(8,128)} %mask.1, bf16[256,256]{1,0:T(8,128)(2,1)} %constant.12.clone.phase, ...), custom_call_target="tpu_custom_call" | custom-call | tf_op jit(solution)/shard_map/gradient/pallas_call | solution.py:563
  374.1 23.0 %wavelet.1 = f32[2,2048,128]{2,1,0:T(8,128)} custom-call(f32[2,7]{1,0:T(2,128)} %limits.1, f32[2,22,128,128]{3,2,1,0:T(8,128)} %gradient.1.descent), custom_call_target="tpu_custom_call" | custom-call | tf_op jit(solution)/shard_map/wavelet/pallas_call | solution.py:135

commit v2 on v1

--- a/solution.py
+++ b/solution.py
@@ -83,7 +83,7 @@
 
         if level:
             extent -= 2 ** (level - 1)
-        lax.fori_loop(0, extent, split, 0)
+        lax.fori_loop(0, extent, split, 0, unroll=2)
     for level in reversed(range(levels)):
         offset = 2**level
         first = halo - (offset - 1)
@@ -122,7 +122,7 @@
                     result[t, pl.ds(jnp.maximum(n - halo, 0), cells_y, stride=planes), :] = value
             return 0
 
-        lax.fori_loop(start, stop, advance, 0)
+        lax.fori_loop(start, stop, advance, 0, unroll=2)
 
 
 def wavelet_shrink(source, thresholds, planes):

time: 397 us -> 396 us (level)
  no operation moved by 1% of the time
where the time goes in v2:
time: 396 us
  Pallas kernels  396 us (100%)
    pallas_call x1, Pallas kernels, descent_planes(): pl.pallas_call(functools.partial(gradient_kernel, sizes), out_shape=jax.S...  374 us
    pallas_call x1, Pallas kernels, wavelet_shrink(): pl.pallas_call(functools.partial(wavelet_kernel, levels, planes), out_sha...  21.8 us

profile of v2, /device:TPU:28, one launch (start us, length us, event | category | flops | bytes accessed | tf_op | source)
XLA Modules:
  0.0 395.9 jit_solution(9612462989982079592)
XLA Ops:
  0.0 374.1 %gradient.1.descent = f32[2,22,128,128]{3,2,1,0:T(8,128)} custom-call(f32[2,2048,128]{2,1,0:T(8,128)} %bitcast.4, bf16[2,8,2048,128]{3,2,1,0:T(8,128)(2,1)} %bitcast.3, bf16[2,8,8,256,128]{4,3,2,1,0:T(8,128)(2,1)} %measured.1, s32[8,256]{1,0:T(8,128)} %mask.1, bf16[256,256]{1,0:T(8,128)(2,1)} %constant.12.clone.phase, ...), custom_call_target="tpu_custom_call" | custom-call | tf_op jit(solution)/shard_map/gradient/pallas_call | solution.py:563
  374.1 21.8 %wavelet.1 = f32[2,2048,128]{2,1,0:T(8,128)} custom-call(f32[2,7]{1,0:T(2,128)} %limits.1, f32[2,22,128,128]{3,2,1,0:T(8,128)} %gradient.1.descent), custom_call_target="tpu_custom_call" | custom-call | tf_op jit(solution)/shard_map/wavelet/pallas_call | solution.py:135
